TPU v7x, 32 devices: a whole 2x2x4 slice. The times are simulated.
32 devices in a mesh: fsdp: 4 (over y, core), sp: 8 (over z, x).
Axes of the slice: x: 2, y: 2, z: 4, core: 2. Of those that a mesh axis runs over, the one named last changes fastest.
Arguments:
- hidden: bfloat16 [4, 2048, 5120], P('fsdp', 'sp'), may hold values from -6 to 6
- queries: bfloat16 [4, 2048, 4096], P('fsdp', 'sp'), may hold values from -240 to 240
- norm_gain: float32 [5120], replicated, may hold values from 0.5 to 1.5
- kv_weight: bfloat16 [5120, 2048], P('fsdp'), may hold values from -0.078125 to 0.078125
- value_bias: float32 [1024], replicated, may hold values from -3 to 3
- doc_lengths: int32 [4, 16], P('fsdp'), may hold values from 1 to 512, 2048 in all within a row
Outputs:
- attended: bfloat16 [4, 2048, 4096], P('fsdp', 'sp')
Inputs may be any that keep to these rules, and one draw needn't show every extreme that they name: `doc_lengths`: each row sums to 2048 and its largest entry is 512.
All inputs are finite; a program needn't handle non-finite values.
Results may differ from a plain program's by a relative error of at most 0.0067.
Values may be sent and summed in bfloat16 or wider, within the bound.
A program may use at most 128 MiB of HBM per device.

v0:
```python
import jax
import jax.numpy as jnp
from jax import lax
from jax.sharding import PartitionSpec as P

QH = 32
KVH = 8
HD = 128


EPS = 1e-06


def from_behind(value, axis, by):
    count = lax.axis_size(axis)
    pairs = [(i, i + by) for i in range(count) if 0 <= i + by < count]
    return lax.ppermute(value, axis, pairs)


def attend_near(query_rows, key_all, value_all, query_pos, key_pos, query_ids, key_ids):
    token_count = query_rows.shape[0]
    ratio = QH // KVH
    scale = HD ** (-0.5)
    allowed = (
        (key_pos[None, :] >= 0)
        & (key_pos[None, :] <= query_pos[:, None])
        & (key_ids[None, :] == query_ids[:, None])
    )
    query_groups = jnp.transpose(query_rows.reshape(token_count, KVH, ratio, HD), (1, 0, 2, 3))
    key_groups = jnp.transpose(key_all, (1, 0, 2))
    value_groups = jnp.transpose(value_all, (1, 0, 2))

    def one_group(operands):
        query_one, key_one, value_one = operands
        scores = (
            jnp.einsum("qrd,kd->rqk", query_one, key_one, preferred_element_type=jnp.float32)
            * scale
        )
        scores = jnp.where(allowed[None], scores, -jnp.inf)
        highest = jnp.max(scores, axis=-1, keepdims=True)
        probs = jnp.exp(scores - highest)
        probs = (probs / jnp.sum(probs, axis=-1, keepdims=True)).astype(jnp.bfloat16)
        output = jnp.einsum("rqk,kd->qrd", probs, value_one, preferred_element_type=jnp.float32)
        return output.astype(jnp.bfloat16)

    outputs = lax.map(one_group, (query_groups, key_groups, value_groups))
    return jnp.transpose(outputs, (1, 0, 2, 3)).reshape(token_count, QH * HD)


def shards(hidden, queries, norm_gain, kv_weight, value_bias, doc_lengths):
    token_count = hidden.shape[1]
    group_size = lax.axis_size("sp")
    query_rows = queries[0]
    wide = hidden[0].astype(jnp.float32)
    normed = (
        wide * lax.rsqrt(jnp.mean(wide * wide, axis=-1, keepdims=True) + EPS) * norm_gain
    ).astype(jnp.bfloat16)
    projected = jnp.dot(
        normed,
        lax.all_gather(kv_weight, "fsdp", axis=0, tiled=True),
        preferred_element_type=jnp.float32,
    )
    keys = projected[:, : KVH * HD].astype(jnp.bfloat16).reshape(token_count, KVH, HD)
    values = (
        (projected[:, KVH * HD :] + value_bias).astype(jnp.bfloat16).reshape(token_count, KVH, HD)
    )
    ends = jnp.cumsum(doc_lengths[0])
    reach = group_size // 4
    first = lax.axis_index("sp") * token_count
    key_parts = [keys]
    value_parts = [values]
    for back in range(1, reach + 1):
        key_far, value_far = from_behind((keys, values), "sp", back)
        key_parts.insert(0, key_far)
        value_parts.insert(0, value_far)
    key_all = jnp.concatenate(key_parts, axis=0)
    value_all = jnp.concatenate(value_parts, axis=0)
    query_pos = first + jnp.arange(token_count, dtype=jnp.int32)
    key_pos = first - reach * token_count + jnp.arange(key_all.shape[0], dtype=jnp.int32)
    query_ids = jnp.sum((query_pos[:, None] >= ends[None, :]).astype(jnp.int32), axis=1)
    key_ids = jnp.sum((key_pos[:, None] >= ends[None, :]).astype(jnp.int32), axis=1)
    result = attend_near(query_rows, key_all, value_all, query_pos, key_pos, query_ids, key_ids)
    return result.reshape(1, token_count, QH * HD)


def solution(mesh):
    in_specs = (
        P("fsdp", "sp", None),
        P("fsdp", "sp", None),
        P(),
        P("fsdp", None),
        P(),
        P("fsdp", None),
    )
    out_specs = P("fsdp", "sp", None)
    return jax.shard_map(shards, mesh=mesh, in_specs=in_specs, out_specs=out_specs, check_vma=False)
```

profile of v0, /device:TPU:8, one launch (start us, length us, event | category | flops | bytes accessed | tf_op | source)
XLA Modules:
  0.0 270.5 jit_solution(13247042923140272168)
XLA Ops:
  8.9 132.8 %all-gather.2.cloned.1.call-done = bf16[5120,2048]{1,0:T(8,128)(2,1)} async-done(((bf16[1280,2048]{1,0:T(8,128)(2,1)}), bf16[5120,2048]{1,0:T(8,128)(2,1)}) %all-gather.2.cloned.1.call-update) | async-done | bytes 20971536 | tf_op jit(solution)/shard_map/all_gather | solution.py:60
  141.7 9.9 %fusion.44 = f32[256,2048]{1,0:T(8,128)S(1)} fusion(bf16[5120,2048]{1,0:T(8,128)(2,1)} %all-gather.2.cloned.1.call-done, bf16[1,256,5120]{2,1,0:T(8,128)(2,1)S(1)} %copy-done, f32[5120]{0:T(1024)S(1)} %copy-done.6, f32[256]{0:T(256)S(1)} %add_rsqrt_fusion), kind=kOutput, calls=%fused_computation.36 | convolution fusion | flops 5373952000 | bytes 25711616 | tf_op jit(solution)/shard_map/dot_general | solution.py:58
  151.7 3.5 %collective-permute-start.2 = (bf16[256,8,128]{2,0,1:T(8,128)(2,1)S(1)}, bf16[256,8,128]{2,0,1:T(8,128)(2,1)}, u32[]{:S(2)}, u32[]{:S(2)}) collective-permute-start(bf16[256,8,128]{2,0,1:T(8,128)(2,1)S(1)} %copy_bitcast_fusion), channel_id=1, source_target_pairs={{0,2},{1,3},{2,4},{3,5},{4,6},{5,7},{8,10},{9,11},{10,12},{11,13},... | collective-permute-start | bytes 1572872 | tf_op jit(solution)/shard_map/ppermute | solution.py:17
  155.3 3.4 %collective-permute-start.3 = (bf16[256,8,128]{2,0,1:T(8,128)(2,1)S(1)}, bf16[256,8,128]{2,0,1:T(8,128)(2,1)}, u32[]{:S(2)}, u32[]{:S(2)}) collective-permute-start(bf16[256,8,128]{2,0,1:T(8,128)(2,1)S(1)} %copy_bitcast_fusion), channel_id=1, source_target_pairs={{0,1},{1,2},{2,3},{3,4},{4,5},{5,6},{6,7},{8,9},{9,10},{10,11},{11... | collective-permute-start | bytes 1572872 | tf_op jit(solution)/shard_map/ppermute | solution.py:17
  159.8 3.4 %collective-permute-start = (bf16[256,8,128]{0,2,1:T(8,128)(2,1)}, bf16[256,8,128]{0,2,1:T(8,128)(2,1)S(1)}, u32[]{:S(2)}, u32[]{:S(2)}) collective-permute-start(bf16[256,8,128]{0,2,1:T(8,128)(2,1)} %bitcast.84), channel_id=1, source_target_pairs={{0,2},{1,3},{2,4},{3,5},{4,6},{5,7},{8,10},{9,11},{10,12},{11,13},... | collective-permute-start | bytes 1572872 | tf_op jit(solution)/shard_map/ppermute | solution.py:17
  165.4 2.5 copy.34
  168.7 12.1 %collective-permute-done.3 = bf16[256,8,128]{2,0,1:T(8,128)(2,1)} collective-permute-done((bf16[256,8,128]{2,0,1:T(8,128)(2,1)S(1)}, bf16[256,8,128]{2,0,1:T(8,128)(2,1)}, u32[]{:S(2)}, u32[]{:S(2)}) %collective-permute-start.3) | collective-permute-done | bytes 524320 | tf_op jit(solution)/shard_map/ppermute | solution.py:17
  180.8 2.5 maximum_bitcast_fusion.1
  183.3 19.2 %collective-permute-done.1 = bf16[256,8,128]{0,2,1:T(8,128)(2,1)} collective-permute-done((bf16[256,8,128]{0,2,1:T(8,128)(2,1)}, bf16[256,8,128]{0,2,1:T(8,128)(2,1)}, u32[]{:S(2)}, u32[]{:S(2)}) %collective-permute-start.1) | collective-permute-done | bytes 524320 | tf_op jit(solution)/shard_map/ppermute | solution.py:17
  204.9 55.9 %while.11 = (s32[]{:T(128)}, bf16[8,256,4,128]{1,3,2,0:T(8,128)(2,1)S(1)}, bf16[8,768,128]{1,2,0:T(8,128)(2,1)}, bf16[8,768,128]{2,1,0:T(8,128)(2,1)}, bf16[8,25...) while((s32[]{:T(128)}, ...), condition=%wide.region_7.8_spmd.clone, body=%wide.region_4.7_spmd.clone.sunk | while | flops 408290048 | bytes 7621485 | solution.py:46
  205.6 3.9 %fusion.70 = (f32[4,256]{1,0:T(4,128)S(1)}, f32[4,256,768]{1,2,0:T(8,128)}) fusion(pred[256,768]{0,1:T(8,128)(4,1)S(1)} %compare_and_fusion.2, bf16[8,256,4,128]{1,3,2,0:T(8,128)(2,1)} %get-tuple-element.198, s32[]{:T(128)} %get-tuple-element.183, bf16[8,768,128]{2,1,0:T(8,128)(2,1)} %get-tuple-element.197), kind=kOutput, calls=%fused_computation.53.clone.1 | convolution fusion | flops 204473088 | bytes 3806208 | tf_op jit(solution)/shard_map/while/body/eval_jaxpr/sub | solution.py:41
  212.6 3.9 %fusion.70 = (f32[4,256]{1,0:T(4,128)S(1)}, f32[4,256,768]{1,2,0:T(8,128)}) fusion(pred[256,768]{0,1:T(8,128)(4,1)S(1)} %compare_and_fusion.2, bf16[8,256,4,128]{1,3,2,0:T(8,128)(2,1)} %get-tuple-element.198, s32[]{:T(128)} %get-tuple-element.183, bf16[8,768,128]{2,1,0:T(8,128)(2,1)} %get-tuple-element.197), kind=kOutput, calls=%fused_computation.53.clone.1 | convolution fusion | flops 204473088 | bytes 3806208 | tf_op jit(solution)/shard_map/while/body/eval_jaxpr/sub | solution.py:41
  216.4 2.4 fusion.71
  219.6 3.9 %fusion.70 = (f32[4,256]{1,0:T(4,128)S(1)}, f32[4,256,768]{1,2,0:T(8,128)}) fusion(pred[256,768]{0,1:T(8,128)(4,1)S(1)} %compare_and_fusion.2, bf16[8,256,4,128]{1,3,2,0:T(8,128)(2,1)} %get-tuple-element.198, s32[]{:T(128)} %get-tuple-element.183, bf16[8,768,128]{2,1,0:T(8,128)(2,1)} %get-tuple-element.197), kind=kOutput, calls=%fused_computation.53.clone.1 | convolution fusion | flops 204473088 | bytes 3806208 | tf_op jit(solution)/shard_map/while/body/eval_jaxpr/sub | solution.py:41
  223.4 2.4 fusion.71
  226.6 3.9 %fusion.70 = (f32[4,256]{1,0:T(4,128)S(1)}, f32[4,256,768]{1,2,0:T(8,128)}) fusion(pred[256,768]{0,1:T(8,128)(4,1)S(1)} %compare_and_fusion.2, bf16[8,256,4,128]{1,3,2,0:T(8,128)(2,1)} %get-tuple-element.198, s32[]{:T(128)} %get-tuple-element.183, bf16[8,768,128]{2,1,0:T(8,128)(2,1)} %get-tuple-element.197), kind=kOutput, calls=%fused_computation.53.clone.1 | convolution fusion | flops 204473088 | bytes 3806208 | tf_op jit(solution)/shard_map/while/body/eval_jaxpr/sub | solution.py:41
  233.6 3.9 %fusion.70 = (f32[4,256]{1,0:T(4,128)S(1)}, f32[4,256,768]{1,2,0:T(8,128)}) fusion(pred[256,768]{0,1:T(8,128)(4,1)S(1)} %compare_and_fusion.2, bf16[8,256,4,128]{1,3,2,0:T(8,128)(2,1)} %get-tuple-element.198, s32[]{:T(128)} %get-tuple-element.183, bf16[8,768,128]{2,1,0:T(8,128)(2,1)} %get-tuple-element.197), kind=kOutput, calls=%fused_computation.53.clone.1 | convolution fusion | flops 204473088 | bytes 3806208 | tf_op jit(solution)/shard_map/while/body/eval_jaxpr/sub | solution.py:41
  237.4 2.4 fusion.71
  240.6 3.9 %fusion.70 = (f32[4,256]{1,0:T(4,128)S(1)}, f32[4,256,768]{1,2,0:T(8,128)}) fusion(pred[256,768]{0,1:T(8,128)(4,1)S(1)} %compare_and_fusion.2, bf16[8,256,4,128]{1,3,2,0:T(8,128)(2,1)} %get-tuple-element.198, s32[]{:T(128)} %get-tuple-element.183, bf16[8,768,128]{2,1,0:T(8,128)(2,1)} %get-tuple-element.197), kind=kOutput, calls=%fused_computation.53.clone.1 | convolution fusion | flops 204473088 | bytes 3806208 | tf_op jit(solution)/shard_map/while/body/eval_jaxpr/sub | solution.py:41
  244.4 2.4 fusion.71
  247.6 3.9 %fusion.70 = (f32[4,256]{1,0:T(4,128)S(1)}, f32[4,256,768]{1,2,0:T(8,128)}) fusion(pred[256,768]{0,1:T(8,128)(4,1)S(1)} %compare_and_fusion.2, bf16[8,256,4,128]{1,3,2,0:T(8,128)(2,1)} %get-tuple-element.198, s32[]{:T(128)} %get-tuple-element.183, bf16[8,768,128]{2,1,0:T(8,128)(2,1)} %get-tuple-element.197), kind=kOutput, calls=%fused_computation.53.clone.1 | convolution fusion | flops 204473088 | bytes 3806208 | tf_op jit(solution)/shard_map/while/body/eval_jaxpr/sub | solution.py:41
  254.6 3.9 %fusion.70 = (f32[4,256]{1,0:T(4,128)S(1)}, f32[4,256,768]{1,2,0:T(8,128)}) fusion(pred[256,768]{0,1:T(8,128)(4,1)S(1)} %compare_and_fusion.2, bf16[8,256,4,128]{1,3,2,0:T(8,128)(2,1)} %get-tuple-element.198, s32[]{:T(128)} %get-tuple-element.183, bf16[8,768,128]{2,1,0:T(8,128)(2,1)} %get-tuple-element.197), kind=kOutput, calls=%fused_computation.53.clone.1 | convolution fusion | flops 204473088 | bytes 3806208 | tf_op jit(solution)/shard_map/while/body/eval_jaxpr/sub | solution.py:41
  258.4 2.4 fusion.71
  260.8 2.9 %copy.39 = bf16[1,256,4096]{2,1,0:T(8,128)(2,1)} copy(bf16[1,256,4096]{1,2,0:T(8,128)(2,1)S(1)} %bitcast.83) | data formatting | bytes 4194304 | tf_op jit(solution)/shard_map/reshape;reshape | solution.py:83
  (45 shorter events, 21.7 us)
Async XLA Ops:
  6.5 1.7 copy-start
  6.5 135.1 %all-gather.2.cloned.1.call-start = ((), (), s32[]{:S(2)}) async-start(), calls=%async_computation | async-start | bytes 26214400 | tf_op jit(solution)/shard_map/all_gather | solution.py:60
  7.3 134.4 %copy-start.6 = (f32[5120]{0:T(1024)S(1)}, f32[5120]{0:T(1024)}, u32[]{:S(2)}) copy-start(f32[5120]{0:T(1024)} %param.10) | copy-start | bytes 61444
  8.9 149.8 %copy-start.4 = (f32[1024]{0:T(1024)S(1)}, f32[1024]{0:T(1024)}, u32[]{:S(2)}) copy-start(f32[1024]{0:T(1024)} %param.12) | copy-start | bytes 12292
  151.6 13.5 %copy-start.5 = (s32[1,16]{1,0:T(1,128)S(1)}, s32[1,16]{1,0:T(1,128)}, u32[]{:S(2)}) copy-start(s32[1,16]{1,0:T(1,128)} %param.13) | copy-start | bytes 196
  151.7 13.7 %copy-start.1 = (bf16[1,256,4096]{2,1,0:T(8,128)(2,1)S(1)}, bf16[1,256,4096]{2,1,0:T(8,128)(2,1)}, u32[]{:S(2)}) copy-start(bf16[1,256,4096]{2,1,0:T(8,128)(2,1)} %param.9) | copy-start | bytes 6291460
  151.7 16.9 %collective-permute-start.2 = (bf16[256,8,128]{2,0,1:T(8,128)(2,1)S(1)}, bf16[256,8,128]{2,0,1:T(8,128)(2,1)}, u32[]{:S(2)}, u32[]{:S(2)}) collective-permute-start(bf16[256,8,128]{2,0,1:T(8,128)(2,1)S(1)} %copy_bitcast_fusion), channel_id=1, source_target_pairs={{0,2},{1,3},{2,4},{3,5},{4,6},{5,7},{8,10},{9,11},{10,12},{11,13},... | collective-permute-start | bytes 1572872 | tf_op jit(solution)/shard_map/ppermute | solution.py:17
  155.3 25.5 %collective-permute-start.3 = (bf16[256,8,128]{2,0,1:T(8,128)(2,1)S(1)}, bf16[256,8,128]{2,0,1:T(8,128)(2,1)}, u32[]{:S(2)}, u32[]{:S(2)}) collective-permute-start(bf16[256,8,128]{2,0,1:T(8,128)(2,1)S(1)} %copy_bitcast_fusion), channel_id=1, source_target_pairs={{0,1},{1,2},{2,3},{3,4},{4,5},{5,6},{6,7},{8,9},{9,10},{10,11},{11... | collective-permute-start | bytes 1572872 | tf_op jit(solution)/shard_map/ppermute | solution.py:17
  159.8 23.5 %collective-permute-start = (bf16[256,8,128]{0,2,1:T(8,128)(2,1)}, bf16[256,8,128]{0,2,1:T(8,128)(2,1)S(1)}, u32[]{:S(2)}, u32[]{:S(2)}) collective-permute-start(bf16[256,8,128]{0,2,1:T(8,128)(2,1)} %bitcast.84), channel_id=1, source_target_pairs={{0,2},{1,3},{2,4},{3,5},{4,6},{5,7},{8,10},{9,11},{10,12},{11,13},... | collective-permute-start | bytes 1572872 | tf_op jit(solution)/shard_map/ppermute | solution.py:17
  163.2 39.4 %collective-permute-start.1 = (bf16[256,8,128]{0,2,1:T(8,128)(2,1)}, bf16[256,8,128]{0,2,1:T(8,128)(2,1)}, u32[]{:S(2)}, u32[]{:S(2)}) collective-permute-start(bf16[256,8,128]{0,2,1:T(8,128)(2,1)} %bitcast.85), channel_id=1, source_target_pairs={{0,1},{1,2},{2,3},{3,4},{4,5},{5,6},{6,7},{8,9},{9,10},{10,11},{11... | collective-permute-start | bytes 1572872 | tf_op jit(solution)/shard_map/ppermute | solution.py:17
  167.9 34.7 %copy-start.3 = (bf16[256,1024]{0,1:T(8,128)(2,1)S(1)}, bf16[256,1024]{0,1:T(8,128)(2,1)}, u32[]{:S(2)}) copy-start(bf16[256,1024]{0,1:T(8,128)(2,1)} %copy.40) | copy-start | bytes 1572868
  168.1 36.8 %copy-start.2 = (bf16[8,256,4,128]{1,3,2,0:T(8,128)(2,1)S(1)}, bf16[8,256,4,128]{1,3,2,0:T(8,128)(2,1)}, u32[]{:S(2)}) copy-start(bf16[8,256,4,128]{1,3,2,0:T(8,128)(2,1)} %custom-call) | copy-start | bytes 6291460
Sparse Core Ops, SparseCore 0:
  8.9 132.7 all-gather.1
where the time goes:
time: 271 us
  waiting for transfers between devices  165 us (61%)
  matrix products  59.9 us (22%)
  between operations  13.5 us (5%)
  starting transfers between devices  12.2 us (5%)
  other arithmetic  11.6 us (4%)
  local copies, waits for them, and re-layouts  7.56 us (3%)
    all_gather x1, waiting for transfers between devices, shards(): lax.all_gather(kv_weight, 'fsdp', axis=0, tiled=True)  133 us
    ppermute x4, waiting for transfers between devices, from_behind(): return lax.ppermute(value, axis, pairs)  32 us
    sub x8, matrix products, one_group(): probs = jnp.exp(scores - highest)  30.8 us
    dot_general x8, matrix products, one_group(): jnp.einsum('rqk,kd->qrd', probs, value_one, preferred_element_type=jnp.fl...  19.1 us
    ppermute x4, starting transfers between devices, from_behind(): return lax.ppermute(value, axis, pairs)  12.2 us
    dot_general x1, matrix products, shards(): jnp.dot(normed, lax.all_gather(kv_weight, 'fsdp', axis=0, tiled=True), pr...  9.95 us
    and x8, other arithmetic, attend_near(): (key_pos[None, :] >= 0) & (key_pos[None, :] <= query_pos[:, None])  5.76 us
  transfers between devices with their start and end apart: 5, of which 4 were waited for; matrix products, arithmetic and copies ran while one was open for 3% of the time, Pallas kernels for 0%

commit v1 on v0

v1 whole, which is shorter than its diff:
```python
import functools
import math

import jax
import jax.numpy as jnp
from jax import lax
from jax.experimental import pallas as pl
from jax.experimental.pallas import tpu as pltpu
from jax.sharding import PartitionSpec as P

QH = 32
KVH = 8
HD = 128
EPS = 1e-06
PAIR = 2 * HD
CHUNKS = KVH // 2
MSGS = 2 * CHUNKS
XCH = 4
QB = 128
MASKED = -1e30


def kernel(
    n, s, reach,
    x_hbm, q_hbm, gain_hbm, w_hbm, vbias_hbm, docs,
    out,
    x, q, gain, vbias, w, xs, xr, own, ps, pr, kv, mask,
    local_sem, x_sem, wsem, xsend, xrecv, psend, precv, ssend, srecv, fsend,
):
    tokens, depth = x.shape
    chips = n // 2
    rows = w_hbm.shape[0]
    half = 2 * rows
    mine = lax.axis_index("fsdp")
    i = lax.axis_index("sp")
    core = lax.rem(mine, 2)
    chip = mine // 2
    mate = chip * 2 + (1 - core)
    step = tokens // XCH

    barrier = pltpu.get_barrier_semaphore()
    pl.semaphore_signal(barrier, inc=1, device_id={"fsdp": mate})
    for o in range(1, chips):
        peer = lax.rem(chip + o, chips) * 2 + core
        pl.semaphore_signal(barrier, inc=1, device_id={"fsdp": peer})
    for b in range(1, reach + 1):
        @pl.when(i >= b)
        def _():
            pl.semaphore_signal(barrier, inc=1, device_id={"sp": i - b})

        @pl.when(i + b < s)
        def _():
            pl.semaphore_signal(barrier, inc=1, device_id={"sp": i + b})

    def xcopy(c):
        part = pl.ds(c * step, step)
        return pltpu.make_async_copy(x_hbm.at[part], x.at[part], x_sem.at[c])

    gcopy = pltpu.make_async_copy(gain_hbm, gain, local_sem.at[0])
    gcopy.start()
    for c in range(XCH):
        xcopy(c).start()
    wcopy = pltpu.make_async_copy(w_hbm, w.at[core], local_sem.at[1])
    wcopy.start()
    qcopy = pltpu.make_async_copy(q_hbm, q, local_sem.at[2])
    qcopy.start()
    bcopy = pltpu.make_async_copy(vbias_hbm, vbias, local_sem.at[3])
    bcopy.start()

    def wsend():
        return pltpu.make_async_remote_copy(
            w_hbm, w.at[core], wsem.at[0], wsem.at[1], device_id={"fsdp": mate}
        )

    def xsendcopy(o, c):
        target = lax.rem(chip + o, chips)
        part = pl.ds(c * step, step)
        return pltpu.make_async_remote_copy(
            xs.at[target, part], xr.at[o - 1, part], xsend.at[o - 1, c], xrecv.at[o - 1, c],
            device_id={"fsdp": target * 2 + core},
        )

    gcopy.wait()
    for c in range(XCH):
        xcopy(c).wait()
        part = slice(c * step, (c + 1) * step)
        wide = x[part, :].astype(jnp.float32)
        inv = lax.rsqrt(jnp.mean(wide * wide, axis=-1, keepdims=True) + EPS)
        for t in range(chips):
            piece = x[part, t * half:(t + 1) * half].astype(jnp.float32)
            piece = piece * inv * gain[:, t * half:(t + 1) * half]
            xs[t, part, :] = piece.astype(jnp.bfloat16)
        if c == 0:
            near = jnp.minimum(i, reach) + jnp.minimum(s - 1 - i, reach)
            pl.semaphore_wait(barrier, chips + near)
        for o in range(1, chips):
            xsendcopy(o, c).start()
        if c == 0:
            wsend().start()

    first = i * tokens
    width = reach * tokens + QB
    for u in range(tokens // QB):
        pos = first + u * QB + lax.broadcasted_iota(jnp.int32, (QB, 1), 0)
        start = jnp.zeros((QB, 1), jnp.int32)
        end = jnp.int32(0)
        for d in range(docs.shape[1]):
            end = end + docs[0, d]
            start = jnp.where(pos >= end, end, start)
        key = first + u * QB - reach * tokens + lax.broadcasted_iota(jnp.int32, (QB, width), 1)
        mask[u] = jnp.where((key >= start) & (key <= pos), 0.0, MASKED)
    for b in range(1, reach + 1):
        @pl.when(i < b)
        def _():
            kv[:, (reach - b) * tokens:(reach - b + 1) * tokens, :] = jnp.zeros(
                (MSGS, tokens, PAIR), jnp.bfloat16
            )

    def columns(m):
        return pl.multiple_of(lax.rem(m, 2) * (KVH * HD) + (m // 2) * PAIR, PAIR)

    def project(left, m):
        cols = pl.ds(columns(m), PAIR)
        total = jnp.dot(left[:, :rows], w[0, :, cols], preferred_element_type=jnp.float32)
        return total + jnp.dot(
            left[:, rows:], w[1, :, cols], preferred_element_type=jnp.float32
        )

    wcopy.wait()
    wsend().wait()
    bcopy.wait()
    qcopy.wait()

    @pl.loop(0, MSGS)
    def _(m):
        shift = vbias[:, pl.ds(pl.multiple_of((m // 2) * PAIR, PAIR), PAIR)]
        shift = shift * lax.rem(m, 2).astype(jnp.float32)
        own[m] = project(xs.at[chip], m) + shift

    def psendcopy(o, m):
        source = lax.rem(chip + chips - o, chips)
        return pltpu.make_async_remote_copy(
            ps.at[o - 1, m], pr.at[o - 1, m], psend.at[o - 1, m], precv.at[o - 1, m],
            device_id={"fsdp": source * 2 + core},
        )

    for o in range(1, chips):
        for c in range(XCH):
            xsendcopy(o, c).wait_recv()

    @pl.loop(0, MSGS)
    def _(m):
        for o in range(1, chips):
            ps[o - 1, m] = project(xr.at[o - 1], m).astype(jnp.bfloat16)
            psendcopy(o, m).start()

    def slot(b):
        return pl.ds((reach - b) * tokens, tokens)

    def shiftcopy(b, m):
        return pltpu.make_async_remote_copy(
            kv.at[m, slot(0)], kv.at[m, slot(b)], ssend.at[b - 1, m], srecv.at[b - 1, m],
            device_id={"sp": i + b},
        )

    def relay(m):
        return pltpu.make_async_remote_copy(
            kv.at[m, slot(2)], kv.at[m, slot(1)], fsend.at[m], srecv.at[0, m],
            device_id={"sp": i - 1},
        )

    odd = lax.rem(i, 2) == 1

    def sends(b):
        return (i + b < s) & jnp.logical_not(odd) if b == 1 else i + b < s

    def finish(m):
        total = own[m]
        for o in range(1, chips):
            psendcopy(o, m).wait_recv()
            total = total + pr[o - 1, m].astype(jnp.float32)
        kv[m, reach * tokens:, :] = total.astype(jnp.bfloat16)
        for b in range(reach, 0, -1):
            @pl.when(sends(b))
            def _():
                shiftcopy(b, m).start()

    def pass_on(m):
        @pl.when(i >= 2)
        def _():
            shiftcopy(2, m).wait_recv()

        @pl.when(odd & (i >= 3))
        def _():
            relay(m).start()

    def arrive(m):
        for b in range(1, reach + 1):
            if b != 2:
                @pl.when(i >= b)
                def _():
                    shiftcopy(b, m).wait_recv()

    factor = HD ** (-0.5) * math.log2(math.e)
    ratio = QH // KVH

    def attend(j):
        for h in range(2):
            for u in range(tokens // QB):
                base = pl.multiple_of((2 * j + h) * ratio * HD, HD)
                left = jnp.concatenate(
                    [q[u * QB:(u + 1) * QB, pl.ds(base + r * HD, HD)] for r in range(ratio)], 0
                )
                keys = kv[2 * j, u * QB:u * QB + width, h * HD:(h + 1) * HD]
                values = kv[2 * j + 1, u * QB:u * QB + width, h * HD:(h + 1) * HD]
                scores = lax.dot_general(
                    left, keys, (((1,), (1,)), ((), ())), preferred_element_type=jnp.float32
                )
                scores = scores.reshape(ratio, QB, width) + mask[u][None]
                scores = scores.reshape(ratio * QB, width)
                highest = jnp.max(scores, axis=-1, keepdims=True)
                probs = jnp.exp2((scores - highest) * factor)
                total = jnp.sum(probs, axis=-1, keepdims=True)
                result = jnp.dot(
                    probs.astype(jnp.bfloat16), values, preferred_element_type=jnp.float32
                )
                result = (result / total).astype(jnp.bfloat16)
                for r in range(ratio):
                    out[u * QB:(u + 1) * QB, pl.ds(base + r * HD, HD)] = result[
                        r * QB:(r + 1) * QB
                    ]

    @pl.loop(0, CHUNKS + 2)
    def _(t):
        @pl.when(t < CHUNKS)
        def _():
            finish(2 * t)
            finish(2 * t + 1)

        @pl.when((t >= 1) & (t < CHUNKS + 1))
        def _():
            pass_on(2 * t - 2)
            pass_on(2 * t - 1)

        @pl.when(t >= 2)
        def _():
            arrive(2 * t - 4)
            arrive(2 * t - 3)
            attend(t - 2)

    for o in range(1, chips):
        for c in range(XCH):
            xsendcopy(o, c).wait_send()

    @pl.loop(0, MSGS)
    def _(m):
        for o in range(1, chips):
            psendcopy(o, m).wait_send()
        for b in range(1, reach + 1):
            @pl.when(sends(b))
            def _():
                shiftcopy(b, m).wait_send()

        @pl.when(odd & (i >= 3))
        def _():
            relay(m).wait_send()


def shards(n, s, hidden, queries, norm_gain, kv_weight, value_bias, doc_lengths):
    _, tokens, depth = hidden.shape
    reach = s // 4
    chips = n // 2
    rows = kv_weight.shape[0]
    far = chips - 1
    vmem = pltpu.VMEM
    dma = pltpu.SemaphoreType.DMA
    anywhere = pl.BlockSpec(memory_space=pl.ANY)
    result = pl.pallas_call(
        functools.partial(kernel, n, s, reach),
        out_shape=jax.ShapeDtypeStruct((tokens, QH * HD), jnp.bfloat16),
        in_specs=[anywhere] * 5 + [pl.BlockSpec(memory_space=pltpu.SMEM)],
        out_specs=pl.BlockSpec(memory_space=pltpu.VMEM),
        scratch_shapes=[
            vmem((tokens, depth), jnp.bfloat16),
            vmem((tokens, QH * HD), jnp.bfloat16),
            vmem((1, depth), jnp.float32),
            vmem((1, KVH * HD), jnp.float32),
            vmem((2, rows, 2 * KVH * HD), jnp.bfloat16),
            vmem((chips, tokens, 2 * rows), jnp.bfloat16),
            vmem((far, tokens, 2 * rows), jnp.bfloat16),
            vmem((MSGS, tokens, PAIR), jnp.float32),
            vmem((far, MSGS, tokens, PAIR), jnp.bfloat16),
            vmem((far, MSGS, tokens, PAIR), jnp.bfloat16),
            vmem((MSGS, (reach + 1) * tokens, PAIR), jnp.bfloat16),
            vmem((tokens // QB, QB, reach * tokens + QB), jnp.float32),
            dma((4,)),
            dma((XCH,)),
            dma((2,)),
            dma((far, XCH)),
            dma((far, XCH)),
            dma((far, MSGS)),
            dma((far, MSGS)),
            dma((reach, MSGS)),
            dma((reach, MSGS)),
            dma((MSGS,)),
        ],
        compiler_params=pltpu.CompilerParams(
            collective_id=0, has_side_effects=True, vmem_limit_bytes=60 * 1024 * 1024
        ),
    )(
        hidden[0], queries[0], norm_gain.reshape(1, depth), kv_weight,
        value_bias.reshape(1, KVH * HD), doc_lengths,
    )
    return result.reshape(1, tokens, QH * HD)


def solution(mesh):
    in_specs = (
        P("fsdp", "sp", None),
        P("fsdp", "sp", None),
        P(),
        P("fsdp", None),
        P(),
        P("fsdp", None),
    )
    body = functools.partial(shards, mesh.shape["fsdp"], mesh.shape["sp"])
    return jax.shard_map(
        body, mesh=mesh, in_specs=in_specs, out_specs=P("fsdp", "sp", None), check_vma=False
    )
```

time: 271 us -> 77.2 us (0.28)
  waiting for transfers between devices: 165 us -> 0 us
  Pallas kernels: 0 us -> 73.9 us
  matrix products: 59.9 us -> 0 us
  between operations: 13.5 us -> 0.01 us
  starting transfers between devices: 12.2 us -> 0 us
  other arithmetic: 11.6 us -> 0 us
  local copies, waits for them, and re-layouts: 7.56 us -> 3.13 us
    all_gather x1 -> x0, waiting for transfers between devices: 133 us -> none  [shards(): lax.all_gather(kv_weight, 'fsdp', axis=0, tiled=True)]
    pallas_call x0 -> x1, Pallas kernels: none -> 73.9 us  [shards(): pl.pallas_call(functools.partial(kernel, n, s, reach), out_shape=jax.Shap...]
    ppermute x4 -> x0, waiting for transfers between devices: 32 us -> none  [from_behind(): return lax.ppermute(value, axis, pairs)]
    sub x8 -> x0, matrix products: 30.8 us -> none  [one_group(): probs = jnp.exp(scores - highest)]
    dot_general x9 -> x0, matrix products: 29.1 us -> none  [the longest x8 19.1 us: one_group(): jnp.einsum('rqk,kd->qrd', probs, value_one, preferred_element_type=jnp.fl...]
    ppermute x4 -> x0, starting transfers between devices: 12.2 us -> none  [from_behind(): return lax.ppermute(value, axis, pairs)]
    and x8 -> x0, other arithmetic: 5.76 us -> none  [attend_near(): (key_pos[None, :] >= 0) & (key_pos[None, :] <= query_pos[:, None])]
    transpose x2 -> x0, other arithmetic: 4.81 us -> none  [the longest x1 2.52 us: attend_near(): key_groups = jnp.transpose(key_all, (1, 0, 2))]
  transfers between devices with their start and end apart: 5 -> 0, of which waited for: 4 -> 0; matrix products, arithmetic and copies ran while one was open for 3% -> 0% of each run, Pallas kernels for 0% -> 0%
where the time goes in v1:
time: 77.2 us; the launch traced here: 77 us
  Pallas kernels  73.9 us (96%)
  local copies, waits for them, and re-layouts  3.13 us (4%)
    pallas_call x1, Pallas kernels, shards(): pl.pallas_call(functools.partial(kernel, n, s, reach), out_shape=jax.Shap...  73.9 us
    unnamed x1, local copies, waits for them, and re-layouts  3.13 us

profile of v1, /device:TPU:8, one launch (start us, length us, event | category | flops | bytes accessed | tf_op | source)
XLA Modules:
  0.0 77.0 jit_solution(617696450153943895)
XLA Ops:
  0.0 73.9 %shard_map.64 = bf16[256,4096]{1,0:T(8,128)(2,1)} custom-call(bf16[256,5120]{1,0:T(8,128)(2,1)} %bitcast.6, bf16[256,4096]{1,0:T(8,128)(2,1)} %bitcast.7, f32[1,5120]{1,0:T(1,128)} %bitcast.8, bf16[1280,2048]{1,0:T(8,128)(2,1)} %w_hbm.1, f32[1,1024]{1,0:T(1,128)} %bitcast.9, s32[1,16]{1,0:T(1,128)} %docs.1), custom_call_target="tpu_custom_call" | custom-call | tf_op jit(solution)/shard_map/pallas_call | solution.py:278
  73.9 3.1 %copy.8 = bf16[1,256,4096]{2,1,0:T(8,128)(2,1)} copy(bf16[1,256,4096]{2,1,0:T(8,128)(2,1)} %bitcast.5) | data formatting | bytes 4194304

commit v2 on v1

--- a/solution.py
+++ b/solution.py
@@ -13,9 +13,9 @@
 HD = 128
 EPS = 1e-06
 PAIR = 2 * HD
-CHUNKS = KVH // 2
-MSGS = 2 * CHUNKS
-XCH = 4
+PAIRS = KVH // 2
+MSGS = 2 * KVH
+XCH = 8
 QB = 128
 MASKED = -1e30
 
@@ -61,11 +61,8 @@
     for c in range(XCH):
         xcopy(c).start()
     wcopy = pltpu.make_async_copy(w_hbm, w.at[core], local_sem.at[1])
-    wcopy.start()
     qcopy = pltpu.make_async_copy(q_hbm, q, local_sem.at[2])
-    qcopy.start()
     bcopy = pltpu.make_async_copy(vbias_hbm, vbias, local_sem.at[3])
-    bcopy.start()
 
     def wsend():
         return pltpu.make_async_remote_copy(
@@ -97,6 +94,9 @@
             xsendcopy(o, c).start()
         if c == 0:
             wsend().start()
+            wcopy.start()
+            bcopy.start()
+            qcopy.start()
 
     first = i * tokens
     width = reach * tokens + QB
@@ -113,14 +113,11 @@
         @pl.when(i < b)
         def _():
             kv[:, (reach - b) * tokens:(reach - b + 1) * tokens, :] = jnp.zeros(
-                (MSGS, tokens, PAIR), jnp.bfloat16
+                (MSGS, tokens, HD), jnp.bfloat16
             )
 
-    def columns(m):
-        return pl.multiple_of(lax.rem(m, 2) * (KVH * HD) + (m // 2) * PAIR, PAIR)
-
-    def project(left, m):
-        cols = pl.ds(columns(m), PAIR)
+    def project(left, j, kind):
+        cols = pl.ds(pl.multiple_of(kind * (KVH * HD) + j * PAIR, PAIR), PAIR)
         total = jnp.dot(left[:, :rows], w[0, :, cols], preferred_element_type=jnp.float32)
         return total + jnp.dot(
             left[:, rows:], w[1, :, cols], preferred_element_type=jnp.float32
@@ -131,28 +128,48 @@
     bcopy.wait()
     qcopy.wait()
 
-    @pl.loop(0, MSGS)
-    def _(m):
-        shift = vbias[:, pl.ds(pl.multiple_of((m // 2) * PAIR, PAIR), PAIR)]
-        shift = shift * lax.rem(m, 2).astype(jnp.float32)
-        own[m] = project(xs.at[chip], m) + shift
-
-    def psendcopy(o, m):
+    @pl.loop(0, PAIRS)
+    def _(j):
+        keys = project(xs.at[chip], j, 0)
+        values = project(xs.at[chip], j, 1)
+        values = values + vbias[:, pl.ds(pl.multiple_of(j * PAIR, PAIR), PAIR)]
+        for h in range(2):
+            own[4 * j + 2 * h] = keys[:, h * HD:(h + 1) * HD]
+            own[4 * j + 2 * h + 1] = values[:, h * HD:(h + 1) * HD]
+
+    def psendcopy(o, m, part):
         source = lax.rem(chip + chips - o, chips)
         return pltpu.make_async_remote_copy(
-            ps.at[o - 1, m], pr.at[o - 1, m], psend.at[o - 1, m], precv.at[o - 1, m],
+            ps.at[o - 1, m, part], pr.at[o - 1, m, part], psend.at[o - 1, m], precv.at[o - 1, m],
             device_id={"fsdp": source * 2 + core},
         )
 
+    whole = pl.ds(0, tokens)
+
+    def give_back(o, j, part):
+        for kind in range(2):
+            partial = project(xr.at[o - 1, part], j, kind).astype(jnp.bfloat16)
+            for h in range(2):
+                ps[o - 1, 4 * j + 2 * h + kind, part, :] = partial[:, h * HD:(h + 1) * HD]
+        for m in range(4):
+            psendcopy(o, 4 * j + m, part).start()
+
+    ahead = XCH - 2
+    early = pl.ds(0, ahead * step)
+    late = pl.ds(ahead * step, tokens - ahead * step)
     for o in range(1, chips):
-        for c in range(XCH):
+        for c in range(ahead):
             xsendcopy(o, c).wait_recv()
-
-    @pl.loop(0, MSGS)
-    def _(m):
+        give_back(o, 0, early)
+    for o in range(1, chips):
+        for c in range(ahead, XCH):
+            xsendcopy(o, c).wait_recv()
+        give_back(o, 0, late)
+
+    @pl.loop(1, PAIRS)
+    def _(j):
         for o in range(1, chips):
-            ps[o - 1, m] = project(xr.at[o - 1], m).astype(jnp.bfloat16)
-            psendcopy(o, m).start()
+            give_back(o, j, whole)
 
     def slot(b):
         return pl.ds((reach - b) * tokens, tokens)
@@ -177,7 +194,7 @@
     def finish(m):
         total = own[m]
         for o in range(1, chips):
-            psendcopy(o, m).wait_recv()
+            psendcopy(o, m, whole).wait_recv()
             total = total + pr[o - 1, m].astype(jnp.float32)
         kv[m, reach * tokens:, :] = total.astype(jnp.bfloat16)
         for b in range(reach, 0, -1):
@@ -204,43 +221,41 @@
     factor = HD ** (-0.5) * math.log2(math.e)
     ratio = QH // KVH
 
-    def attend(j):
-        for h in range(2):
-            for u in range(tokens // QB):
-                base = pl.multiple_of((2 * j + h) * ratio * HD, HD)
-                left = jnp.concatenate(
-                    [q[u * QB:(u + 1) * QB, pl.ds(base + r * HD, HD)] for r in range(ratio)], 0
-                )
-                keys = kv[2 * j, u * QB:u * QB + width, h * HD:(h + 1) * HD]
-                values = kv[2 * j + 1, u * QB:u * QB + width, h * HD:(h + 1) * HD]
-                scores = lax.dot_general(
-                    left, keys, (((1,), (1,)), ((), ())), preferred_element_type=jnp.float32
-                )
-                scores = scores.reshape(ratio, QB, width) + mask[u][None]
-                scores = scores.reshape(ratio * QB, width)
-                highest = jnp.max(scores, axis=-1, keepdims=True)
-                probs = jnp.exp2((scores - highest) * factor)
-                total = jnp.sum(probs, axis=-1, keepdims=True)
-                result = jnp.dot(
-                    probs.astype(jnp.bfloat16), values, preferred_element_type=jnp.float32
-                )
-                result = (result / total).astype(jnp.bfloat16)
-                for r in range(ratio):
-                    out[u * QB:(u + 1) * QB, pl.ds(base + r * HD, HD)] = result[
-                        r * QB:(r + 1) * QB
-                    ]
-
-    @pl.loop(0, CHUNKS + 2)
+    def attend(g):
+        base = pl.multiple_of(g * ratio * HD, HD)
+        for u in range(tokens // QB):
+            left = jnp.concatenate(
+                [q[u * QB:(u + 1) * QB, pl.ds(base + r * HD, HD)] for r in range(ratio)], 0
+            )
+            keys = kv[2 * g, u * QB:u * QB + width, :]
+            values = kv[2 * g + 1, u * QB:u * QB + width, :]
+            scores = lax.dot_general(
+                left, keys, (((1,), (1,)), ((), ())), preferred_element_type=jnp.float32
+            )
+            scores = scores.reshape(ratio, QB, width) + mask[u][None]
+            scores = scores.reshape(ratio * QB, width)
+            highest = jnp.max(scores, axis=-1, keepdims=True)
+            probs = jnp.exp2((scores - highest) * factor)
+            total = jnp.sum(probs, axis=-1, keepdims=True)
+            result = jnp.dot(
+                probs.astype(jnp.bfloat16), values, preferred_element_type=jnp.float32
+            )
+            result = (result / total).astype(jnp.bfloat16)
+            for r in range(ratio):
+                out[u * QB:(u + 1) * QB, pl.ds(base + r * HD, HD)] = result[
+                    r * QB:(r + 1) * QB
+                ]
+
+    @pl.loop(0, KVH + 2)
     def _(t):
-        @pl.when(t < CHUNKS)
-        def _():
-            finish(2 * t)
-            finish(2 * t + 1)
-
-        @pl.when((t >= 1) & (t < CHUNKS + 1))
-        def _():
-            pass_on(2 * t - 2)
-            pass_on(2 * t - 1)
+        for kind in range(2):
+            @pl.when(t < KVH)
+            def _():
+                finish(2 * t + kind)
+
+            @pl.when((t >= 1) & (t < KVH + 1))
+            def _():
+                pass_on(2 * t - 2 + kind)
 
         @pl.when(t >= 2)
         def _():
@@ -255,7 +270,7 @@
     @pl.loop(0, MSGS)
     def _(m):
         for o in range(1, chips):
-            psendcopy(o, m).wait_send()
+            psendcopy(o, m, whole).wait_send()
         for b in range(1, reach + 1):
             @pl.when(sends(b))
             def _():
@@ -274,7 +289,7 @@
     far = chips - 1
     vmem = pltpu.VMEM
     dma = pltpu.SemaphoreType.DMA
-    anywhere = pl.BlockSpec(memory_space=pl.ANY)
+    anywhere = pl.BlockSpec(memory_space=pltpu.HBM)
     result = pl.pallas_call(
         functools.partial(kernel, n, s, reach),
         out_shape=jax.ShapeDtypeStruct((tokens, QH * HD), jnp.bfloat16),
@@ -288,10 +303,10 @@
             vmem((2, rows, 2 * KVH * HD), jnp.bfloat16),
             vmem((chips, tokens, 2 * rows), jnp.bfloat16),
             vmem((far, tokens, 2 * rows), jnp.bfloat16),
-            vmem((MSGS, tokens, PAIR), jnp.float32),
-            vmem((far, MSGS, tokens, PAIR), jnp.bfloat16),
-            vmem((far, MSGS, tokens, PAIR), jnp.bfloat16),
-            vmem((MSGS, (reach + 1) * tokens, PAIR), jnp.bfloat16),
+            vmem((MSGS, tokens, HD), jnp.float32),
+            vmem((far, MSGS, tokens, HD), jnp.bfloat16),
+            vmem((far, MSGS, tokens, HD), jnp.bfloat16),
+            vmem((MSGS, (reach + 1) * tokens, HD), jnp.bfloat16),
             vmem((tokens // QB, QB, reach * tokens + QB), jnp.float32),
             dma((4,)),
             dma((XCH,)),
@@ -305,7 +320,7 @@
             dma((MSGS,)),
         ],
         compiler_params=pltpu.CompilerParams(
-            collective_id=0, has_side_effects=True, vmem_limit_bytes=60 * 1024 * 1024
+            collective_id=0, has_side_effects=True, vmem_limit_bytes=50 * 1024 * 1024
         ),
     )(
         hidden[0], queries[0], norm_gain.reshape(1, depth), kv_weight,

time: 77.2 us -> 72.3 us (0.937); the launches traced: 77 us -> 70.9 us
  Pallas kernels: 73.9 us -> 67.5 us
    pallas_call x1, Pallas kernels: 73.9 us -> 67.5 us  [shards(): pl.pallas_call(functools.partial(kernel, n, s, reach), out_shape=jax.Shap...]
    unnamed x1 -> x7, local copies, waits for them, and re-layouts: 3.13 us -> 3.39 us
where the time goes in v2:
time: 72.3 us; the launch traced here: 70.9 us
  Pallas kernels  67.5 us (93%)
  local copies, waits for them, and re-layouts  3.39 us (5%)
    pallas_call x1, Pallas kernels, shards(): pl.pallas_call(functools.partial(kernel, n, s, reach), out_shape=jax.Shap...  67.5 us
    unnamed x7, local copies, waits for them, and re-layouts  3.39 us

profile of v2, /device:TPU:8, one launch (start us, length us, event | category | flops | bytes accessed | tf_op | source)
XLA Modules:
  0.0 70.9 jit_solution(8885063265529638245)
XLA Ops:
  0.0 0.0 copy-start
  0.0 0.7 %copy-done = f32[5120]{0:T(1024)S(1)} copy-done((f32[5120]{0:T(1024)S(1)}, f32[5120]{0:T(1024)}, u32[]{:S(2)}) %copy-start) | copy-done | bytes 20504
  0.7 0.0 copy-start.1
  0.7 0.7 copy-done.1
  1.4 0.0 copy-start.2
  1.4 0.7 copy-done.2
  2.1 67.5 %shard_map.64 = bf16[256,4096]{1,0:T(8,128)(2,1)S(1)} custom-call(bf16[256,5120]{1,0:T(8,128)(2,1)} %bitcast.8, bf16[256,4096]{1,0:T(8,128)(2,1)} %bitcast.9, f32[1,5120]{1,0:T(1,128)S(1)} %bitcast.6, bf16[1280,2048]{1,0:T(8,128)(2,1)} %w_hbm.1, f32[1,1024]{1,0:T(1,128)S(1)} %bitcast.7, s32[1,16]{1,0:T(1,128)S(1)} %copy-done.2), custom_call_target="tpu_custom_call" | custom-call | tf_op jit(solution)/shard_map/pallas_call | solution.py:293
  69.6 1.3 %copy.8 = bf16[1,256,4096]{2,1,0:T(8,128)(2,1)} copy(bf16[1,256,4096]{2,1,0:T(8,128)(2,1)S(1)} %bitcast.5) | data formatting | bytes 4194304
Async XLA Ops:
  0.0 0.7 %copy-start = (f32[5120]{0:T(1024)S(1)}, f32[5120]{0:T(1024)}, u32[]{:S(2)}) copy-start(f32[5120]{0:T(1024)} %param.8) | copy-start | bytes 61444
  0.7 0.7 copy-start.1
  1.4 0.7 copy-start.2
